TPU v7x, 32 devices: a whole 2x2x4 slice. The times are simulated.
32 devices in a mesh: seq: 4 (over y, x), exp: 8 (over z, core), dp: 1.
Axes of the slice: x: 2, y: 2, z: 4, core: 2. Of those that a mesh axis runs over, the one named last changes fastest.
Arguments:
- tokens: bfloat16 [8, 16, 64, 1280], P(('dp', 'exp'), 'seq'), may hold values from -6 to 6
- expert_ids: int32 [8, 16, 64, 1], P(('dp', 'exp'), 'seq'), may hold values from 0 to 15; in each aligned block of 256 rows (0 to 255, 256 to 511, ..., all dimensions but the last counted through in order) at most 20 rows name the same one
- gate_values: float32 [8, 16, 64], P(('dp', 'exp'), 'seq'), may hold values from 0.25 to 1
- mixer_gain: float32 [1280], replicated, may hold values from 0.1 to 1.9
- expert_gain: float32 [1280], replicated, may hold values from 0.1 to 1.9
- conv_weight: float32 [3, 3, 1280], replicated, may hold values from -2 to 2
- conv_bias: float32 [1280], replicated, may hold values from -3 to 3
- w_in: bfloat16 [16, 1280, 5120], P('exp', None, 'seq'), may hold values from -0.15625 to 0.15625
- b_in: float32 [16, 5120], P('exp', 'seq'), may hold values from -3 to 3
- w_out: bfloat16 [16, 5120, 1280], P('exp', 'seq'), may hold values from -0.078125 to 0.078125
- b_out: float32 [16, 1280], P('exp'), may hold values from -3 to 3
Outputs:
- result: bfloat16 [8, 16, 64, 1280], P(('dp', 'exp'), 'seq')
Inputs may be any that keep to these rules, and one draw needn't show every extreme that they name: `expert_ids`: among the 256 patches of one image's block of 4 rows (rows k * 4 to k * 4 + 3), no expert is chosen more than 20 times, and in every draw some expert is chosen exactly 20 times in some block.
All inputs are finite; a program needn't handle non-finite values.
Results may differ from a plain program's by a relative error of at most 0.006.
Values may be sent and summed in bfloat16 or wider, within the bound.
A program may use at most 128 MiB of HBM per device.

v0:
```python
import jax
import jax.numpy as jnp
from jax import lax
from jax.sharding import PartitionSpec as P


def with_halo(cells, sides, width):
    for axis, dim in sides:
        count = lax.axis_size(axis)
        ends = count - 1
        head = lax.slice_in_dim(cells, 0, width, axis=dim)
        tail = lax.slice_in_dim(cells, cells.shape[dim] - width, cells.shape[dim], axis=dim)
        cells = jnp.concatenate(
            [
                lax.ppermute(tail, axis, [(i, (i + 1) % count) for i in range(ends)]),
                cells,
                lax.ppermute(head, axis, [((i + 1) % count, i) for i in range(ends)]),
            ],
            axis=dim,
        )
    return cells


def normalize(values, scales):
    row_mean = jnp.mean(values, axis=-1, keepdims=True)
    centred = values - row_mean
    row_var = jnp.mean(centred * centred, axis=-1, keepdims=True)
    return centred * lax.rsqrt(row_var + 1e-06) * scales


def depthwise(padded, conv_weight, height, width):
    summed = padded[..., 0:height, 0:width, :] * conv_weight[0, 0]
    for row_off in range(3):
        for col_off in range(3):
            if row_off + col_off > 0:
                summed = (
                    summed
                    + padded[..., row_off : row_off + height, col_off : col_off + width, :]
                    * conv_weight[row_off, col_off]
                )
    return summed


def body(
    tokens,
    expert_ids,
    gate_values,
    mixer_gain,
    expert_gain,
    conv_weight,
    conv_bias,
    w_in,
    b_in,
    w_out,
    b_out,
):
    row_count = tokens.shape[1]
    col_count = tokens.shape[2]
    width_d = tokens.shape[3]
    values = tokens[0].astype(jnp.float32)
    normed = normalize(values, mixer_gain).astype(jnp.bfloat16)
    rim_source = tokens[0]
    extended = with_halo(rim_source, (("seq", 0),), 1)
    rim_rows = jnp.concatenate([extended[0:1], extended[row_count + 1 : row_count + 2]], axis=0)
    rim_rows = normalize(rim_rows.astype(jnp.float32), mixer_gain).astype(jnp.bfloat16)
    extended = jnp.concatenate([rim_rows[0:1], normed, rim_rows[1:2]], axis=0)
    padded = jnp.pad(extended.astype(jnp.float32), ((0, 0), (1, 1), (0, 0)))
    mixed = values + depthwise(padded, conv_weight, row_count, col_count) + conv_bias
    tok_rows = row_count * col_count
    expert_in = normalize(mixed, expert_gain).astype(jnp.bfloat16).reshape(tok_rows, width_d)
    per_device = w_in.shape[0]
    holders = lax.axis_size("exp")
    experts = per_device * holders
    slot_count = 5 * tok_rows // (4 * experts)
    route_ids = expert_ids.reshape(tok_rows)
    one_hot = (route_ids[:, None] == jnp.arange(experts, dtype=jnp.int32)[None, :]).astype(
        jnp.float32
    )
    positions = jnp.arange(tok_rows, dtype=jnp.int32)
    below_mask = (positions[:, None] > positions[None, :]).astype(jnp.float32)
    earlier = jnp.dot(below_mask, one_hot, precision=lax.Precision.HIGHEST)
    slot_rank = jnp.sum(earlier * one_hot, axis=1).astype(jnp.int32)
    column = (
        route_ids // per_device * slot_count + slot_rank
    ) * per_device + route_ids % per_device
    dispatch_mask = (
        column[:, None] == jnp.arange(experts * slot_count, dtype=jnp.int32)[None, :]
    ).astype(jnp.bfloat16)
    dispatched = jnp.einsum(
        "tk,td->kd", dispatch_mask, expert_in, preferred_element_type=jnp.float32
    ).astype(jnp.bfloat16)
    dispatched = dispatched.reshape(holders, slot_count, per_device, width_d)
    received = lax.all_to_all(dispatched, "exp", split_axis=0, concat_axis=0, tiled=True)
    gathered = lax.all_gather(received, "seq", axis=0, tiled=True)
    hidden = (
        jnp.einsum("kcjd,jdf->kcjf", gathered, w_in, preferred_element_type=jnp.float32)
        + b_in[None, None]
    )
    hidden = jax.nn.gelu(hidden, approximate=False).astype(jnp.bfloat16)
    summed = lax.psum_scatter(
        jnp.einsum("kcjf,jfd->kcjd", hidden, w_out, preferred_element_type=jnp.float32).astype(
            jnp.bfloat16
        ),
        "seq",
        scatter_dimension=0,
        tiled=True,
    ).astype(jnp.float32)
    back = (summed + b_out[None, None]).astype(jnp.bfloat16)
    returned = lax.all_to_all(back, "exp", split_axis=0, concat_axis=0, tiled=True).reshape(
        experts * slot_count, width_d
    )
    combined = jnp.dot(dispatch_mask, returned, preferred_element_type=jnp.float32)
    result = mixed.reshape(tok_rows, width_d) + gate_values.reshape(tok_rows)[:, None] * combined
    return result.astype(jnp.bfloat16).reshape(tokens.shape)


def solution(mesh):
    in_specs = (
        P(("dp", "exp"), "seq", None, None),
        P(("dp", "exp"), "seq", None, None),
        P(("dp", "exp"), "seq", None),
        P(),
        P(),
        P(),
        P(),
        P("exp", None, "seq"),
        P("exp", "seq"),
        P("exp", "seq", None),
        P("exp", None),
    )
    out_specs = P(("dp", "exp"), "seq", None, None)
    return jax.shard_map(body, mesh=mesh, in_specs=in_specs, out_specs=out_specs, check_vma=False)
```

profile of v0, /device:TPU:1, one launch (start us, length us, event | category | flops | bytes accessed | tf_op | source)
XLA Modules:
  0.0 250.3 jit_solution(8246622316100083128)
XLA Ops:
  6.5 1.1 slice_bitcast_fusion.1
  7.6 3.9 %collective-permute-start = (bf16[1,64,1280]{2,1,0:T(8,128)(2,1)S(1)}, bf16[1,64,1280]{2,1,0:T(8,128)(2,1)S(1)}, u32[]{:S(2)}, u32[]{:S(2)}) collective-permute-start(bf16[1,64,1280]{2,1,0:T(8,128)(2,1)S(1)} %get-tuple-element.16), channel_id=1, source_target_pairs={{0,8},{8,16},{16,24},{1,9},{9,17},{17,25},{2,10},{10,18},{18,26},{... | collective-permute-start | bytes 491528 | tf_op jit(solution)/shard_map/ppermute | solution.py:15
  11.6 1.3 collective-permute-start.1
  12.9 1.3 convert_reduce_fusion
  14.1 1.4 fusion.53
  15.6 0.5 broadcast.173
  16.1 1.3 reduce.22
  17.7 1.4 fusion.55
  19.1 1.0 slice_reduce_fusion.8
  20.5 0.9 fusion.76
  21.7 1.8 fusion.111
  24.1 0.5 convolution_convert_fusion
  24.6 0.3 reshape.122
  24.9 27.0 %all_to_all.10 = bf16[8,20,2,1280]{3,2,1,0:T(2,128)(2,1)S(1)} all-to-all(bf16[8,20,2,1280]{3,2,1,0:T(2,128)(2,1)S(1)} %reshape.122), channel_id=1, replica_groups=mesh['seq'=4,'exp'=8,'dp'=1] {'exp'}, dimensions={0} | all-to-all | bytes 1638400 | tf_op jit(solution)/shard_map/all_to_all | solution.py:93
  52.0 1.0 copy.19
  53.3 44.4 %all-gather.2.cloned.1.call-done = bf16[32,20,2,1280]{3,0,1,2:T(8,128)(2,1)} async-done(((bf16[8,20,2,1280]{3,0,1,2:T(8,128)(2,1)}), bf16[32,20,2,1280]{3,0,1,2:T(8,128)(2,1)}) %all-gather.2.cloned.1.call-update) | async-done | bytes 3276816 | tf_op jit(solution)/shard_map/all_gather | solution.py:94
  97.6 25.7 %fusion.27 = bf16[32,20,2,1280]{3,0,1,2:T(8,128)(2,1)} fusion(bf16[2,1280,1280]{2,1,0:T(8,128)(2,1)} %param.20, bf16[32,20,2,1280]{3,0,1,2:T(8,128)(2,1)} %all-gather.2.cloned.1.call-done, bf16[2,1280,1280]{2,1,0:T(8,128)(2,1)} %param.18, f32[2,1280]{1,0:T(2,128)S(1)} %copy-done.5), kind=kOutput, calls=%fused_computation.29 | convolution fusion | flops 8498380800 | bytes 19671040 | tf_op jit(solution)/shard_map/kcjf,jfd->kcjd/dot_general | solution.py:101
  123.3 0.6 dynamic-slice
  124.6 88.0 %all-reduce.4.cloned.1.call-done = bf16[32,20,2,1280]{3,0,1,2:T(8,128)(2,1)} async-done(((bf16[32,20,2,1280]{3,0,1,2:T(8,128)(2,1)}), bf16[32,20,2,1280]{3,0,1,2:T(8,128)(2,1)}) %all-reduce.4.cloned.1.call-update) | async-done | bytes 3276816
  212.6 1.3 add_convert_fusion
  213.9 1.7 copy.20
  215.6 5.4 %all-to-all-start.1 = ((bf16[8,20,2,1280]{3,2,1,0:T(2,128)(2,1)}), bf16[8,20,2,1280]{3,2,1,0:T(2,128)(2,1)S(1)}, u32[]{:S(2)}, u32[]{:S(2)}) async-start(bf16[8,20,2,1280]{3,2,1,0:T(2,128)(2,1)} %copy.20), calls=%async_computation.1 | async-start | bytes 1638400 | tf_op jit(solution)/shard_map/all_to_all | solution.py:109
  221.2 20.6 %all-to-all-done.1 = bf16[8,20,2,1280]{3,2,1,0:T(2,128)(2,1)S(1)} async-done(((bf16[8,20,2,1280]{3,2,1,0:T(2,128)(2,1)}), bf16[8,20,2,1280]{3,2,1,0:T(2,128)(2,1)S(1)}, u32[]{:S(2)}, u32[]{:S(2)}) %all-to-all-start.1) | async-done | bytes 819232 | tf_op jit(solution)/shard_map/all_to_all | solution.py:109
  242.1 1.4 fusion.48
  (37 shorter events, 2.1 us)
Async XLA Ops:
  6.5 15.2 %copy-start = (bf16[1,4,64,1280]{3,2,1,0:T(8,128)(2,1)S(1)}, bf16[1,4,64,1280]{3,2,1,0:T(8,128)(2,1)}, u32[]{:S(2)}) copy-start(bf16[1,4,64,1280]{3,2,1,0:T(8,128)(2,1)} %param.11) | copy-start | bytes 1966084
  6.5 15.2 %copy-start.3 = (f32[1280]{0:T(1024)S(1)}, f32[1280]{0:T(1024)}, u32[]{:S(2)}) copy-start(f32[1280]{0:T(1024)} %param.17) | copy-start | bytes 15364
  6.5 91.1 %all-gather.2.cloned.1.call-start = ((), (), s32[]{:S(2)}) async-start(), calls=%async_computation.2 | async-start | bytes 4096000 | tf_op jit(solution)/shard_map/all_gather | solution.py:94
  7.6 12.5 %collective-permute-start = (bf16[1,64,1280]{2,1,0:T(8,128)(2,1)S(1)}, bf16[1,64,1280]{2,1,0:T(8,128)(2,1)S(1)}, u32[]{:S(2)}, u32[]{:S(2)}) collective-permute-start(bf16[1,64,1280]{2,1,0:T(8,128)(2,1)S(1)} %get-tuple-element.16), channel_id=1, source_target_pairs={{0,8},{8,16},{16,24},{1,9},{9,17},{17,25},{2,10},{10,18},{18,26},{... | collective-permute-start | bytes 491528 | tf_op jit(solution)/shard_map/ppermute | solution.py:15
  11.6 8.6 %collective-permute-start.1 = (bf16[1,64,1280]{2,1,0:T(8,128)(2,1)S(1)}, bf16[1,64,1280]{2,1,0:T(8,128)(2,1)S(1)}, u32[]{:S(2)}, u32[]{:S(2)}) collective-permute-start(bf16[1,64,1280]{2,1,0:T(8,128)(2,1)S(1)} %get-tuple-element.17), channel_id=1, source_target_pairs={{8,0},{16,8},{24,16},{9,1},{17,9},{25,17},{10,2},{18,10},{26,18},{... | collective-permute-start | bytes 491528 | tf_op jit(solution)/shard_map/ppermute | solution.py:17
  21.5 2.4 copy-start.2
  23.5 74.1 %copy-start.5 = (f32[2,1280]{1,0:T(2,128)S(1)}, f32[2,1280]{1,0:T(2,128)}, u32[]{:S(2)}) copy-start(f32[2,1280]{1,0:T(2,128)} %param.19) | copy-start | bytes 30724
  53.0 70.3 %copy-start.6 = (u32[32]{0:T(128)S(1)}, u32[32]{0:T(128)}, u32[]{:S(2)}) copy-start(u32[32]{0:T(128)} %constant.116) | copy-start | bytes 388
  53.0 159.6 %copy-start.1 = (f32[2,1280]{1,0:T(2,128)S(1)}, f32[2,1280]{1,0:T(2,128)}, u32[]{:S(2)}) copy-start(f32[2,1280]{1,0:T(2,128)} %param.21) | copy-start | bytes 30724
  53.0 159.6 %all-reduce.4.cloned.1.call-start = ((), (), s32[]{:S(2)}) async-start(), calls=%async_computation.3 | async-start | bytes 6553600
  123.3 97.8 %copy-start.4 = (f32[1,4,64]{2,1,0:T(4,128)S(1)}, f32[1,4,64]{2,1,0:T(4,128)}, u32[]{:S(2)}) copy-start(f32[1,4,64]{2,1,0:T(4,128)} %param.13) | copy-start | bytes 3076
  215.6 26.1 %all-to-all-start.1 = ((bf16[8,20,2,1280]{3,2,1,0:T(2,128)(2,1)}), bf16[8,20,2,1280]{3,2,1,0:T(2,128)(2,1)S(1)}, u32[]{:S(2)}, u32[]{:S(2)}) async-start(bf16[8,20,2,1280]{3,2,1,0:T(2,128)(2,1)} %copy.20), calls=%async_computation.1 | async-start | bytes 1638400 | tf_op jit(solution)/shard_map/all_to_all | solution.py:109
Sparse Core Ops, SparseCore 0:
  53.1 44.4 all-gather.1
  123.4 89.1 all-reduce.3
where the time goes:
time: 252 us; the launch traced here: 250 us
  waiting for transfers between devices  153 us (61%)
  matrix products  27.8 us (11%)
  blocking collectives  27 us (11%)
  between operations  14.2 us (6%)
  starting transfers between devices  10.9 us (4%)
  other arithmetic  10.5 us (4%)
  local copies, waits for them, and re-layouts  6.83 us (3%)
    unnamed x3, waiting for transfers between devices  88.1 us
    all_gather x1, waiting for transfers between devices, body(): gathered = lax.all_gather(received, 'seq', axis=0, tiled=True)  44.4 us
    all_to_all x1, blocking collectives, body(): lax.all_to_all(dispatched, 'exp', split_axis=0, concat_axis=0, tiled=True)  27 us
    dot_general x1, matrix products, body(): jnp.einsum('kcjf,jfd->kcjd', hidden, w_out, preferred_element_type=jnp.fl...  25.7 us
    all_to_all x1, waiting for transfers between devices, body(): lax.all_to_all(back, 'exp', split_axis=0, concat_axis=0, tiled=True)  20.6 us
    all_to_all x1, starting transfers between devices, body(): lax.all_to_all(back, 'exp', split_axis=0, concat_axis=0, tiled=True)  5.44 us
  transfers between devices with their start and end apart: 5, of which 3 were waited for; matrix products, arithmetic and copies ran while one was open for 3% of the time, Pallas kernels for 0%

commit v1 on v0

--- a/solution.py
+++ b/solution.py
@@ -1,6 +1,11 @@
+import functools
+import math
+
 import jax
 import jax.numpy as jnp
 from jax import lax
+from jax.experimental import pallas as pl
+from jax.experimental.pallas import tpu as pltpu
 from jax.sharding import PartitionSpec as P
 
 
@@ -39,6 +44,383 @@
                     * conv_weight[row_off, col_off]
                 )
     return summed
+
+
+VMEM_LIMIT = 62 * 1024 * 1024
+MESH = pl.DeviceIdType.MESH
+
+
+def exchange_kernel(
+    dims,
+    x_ref,
+    b_in_ref,
+    b_out_ref,
+    w_in_ref,
+    w_out_ref,
+    out_ref,
+    w1,
+    w2,
+    buf,
+    part,
+    got1,
+    red,
+    got2,
+    fin,
+    xs,
+    hs,
+    w_sem,
+    own_sem,
+    z_send,
+    z_recv,
+    a1_send,
+    a1_recv,
+    a2_send,
+    a2_recv,
+    r1_send,
+    r1_recv,
+    r2_send,
+    r2_recv,
+    b_send,
+    b_recv,
+):
+    n_seq, n_exp, n_chunk, pair, major, minor, experts, slot = dims
+    groups = x_ref.shape[1]
+    width = x_ref.shape[3]
+    hidden = w1.shape[2]
+    me_s = lax.axis_index("seq")
+    me_e = lax.axis_index("exp")
+    me_z = me_e // pair
+    me_c = me_e % pair
+
+    def place(h):
+        if major == minor and h % 2 == 1:
+            return me_s % minor, me_s // minor
+        return me_s // minor, me_s % minor
+
+    def at(h, maj, low):
+        if major == minor and h % 2 == 1:
+            return low * minor + maj
+        return maj * minor + low
+
+    def remote(src, dst, send, recv, seq, exp):
+        return pltpu.make_async_remote_copy(
+            src_ref=src,
+            dst_ref=dst,
+            send_sem=send,
+            recv_sem=recv,
+            device_id={"seq": seq, "exp": exp},
+            device_id_type=MESH,
+        )
+
+    weights = []
+    for j in range(experts):
+        weights.append(pltpu.make_async_copy(w_in_ref.at[j], w1.at[j], w_sem.at[0, j]))
+    for j in range(experts):
+        weights.append(pltpu.make_async_copy(w_out_ref.at[j], w2.at[j], w_sem.at[1, j]))
+
+    barrier = pltpu.get_barrier_semaphore()
+    greeted = 0
+    for d in range(1, n_exp):
+        pl.semaphore_signal(
+            barrier,
+            inc=1,
+            device_id={"seq": me_s, "exp": (me_e + d) % n_exp},
+            device_id_type=MESH,
+        )
+        greeted += 1
+    for h in range(min(pair, 2) if major == minor else 1):
+        maj, low = place(h)
+        for d in range(1, minor):
+            pl.semaphore_signal(
+                barrier,
+                inc=1,
+                device_id={"seq": at(h, maj, (low + d) % minor), "exp": me_e},
+                device_id_type=MESH,
+            )
+            greeted += 1
+        if pair == 1:
+            for d in range(1, major):
+                pl.semaphore_signal(
+                    barrier,
+                    inc=1,
+                    device_id={"seq": at(h, (maj + d) % major, low), "exp": me_e},
+                    device_id_type=MESH,
+                )
+                greeted += 1
+    pl.semaphore_wait(barrier, greeted)
+
+    def z_copy(c, h):
+        target = (me_z + c) % n_chunk * pair + (me_c + pair - h) % pair
+        maj, low = place(h)
+        return remote(
+            x_ref.at[target],
+            buf.at[c, h, maj, low],
+            z_send.at[c, h],
+            z_recv.at[c, h],
+            me_s,
+            target,
+        )
+
+    own_maj, own_low = place(0)
+    own = pltpu.make_async_copy(x_ref.at[me_e], buf.at[0, 0, own_maj, own_low], own_sem)
+
+    def a1_copy(c, h, d):
+        maj, low = place(h)
+        block = buf.at[c, h, maj, low]
+        return remote(
+            block,
+            block,
+            a1_send.at[c, h, d],
+            a1_recv.at[c, h, d],
+            at(h, maj, (low + d) % minor),
+            me_e,
+        )
+
+    def a2_copy(c, h, d):
+        maj, low = place(h)
+        block = buf.at[c, h, maj]
+        return remote(
+            block,
+            block,
+            a2_send.at[c, h, d],
+            a2_recv.at[c, h, d],
+            at(h, (maj + d) % major, low),
+            me_e,
+        )
+
+    def r1_copy(c, h, d):
+        maj, low = place(h)
+        return remote(
+            part.at[c, h, (maj + d) % major],
+            got1.at[c, h, d - 1],
+            r1_send.at[c, h, d],
+            r1_recv.at[c, h, d],
+            at(h, (maj + d) % major, low),
+            me_e,
+        )
+
+    def r2_copy(c, h, d):
+        maj, low = place(h)
+        return remote(
+            red.at[c, h, (low + d) % minor],
+            got2.at[c, h, d - 1],
+            r2_send.at[c, h, d],
+            r2_recv.at[c, h, d],
+            at(h, maj, (low + d) % minor),
+            me_e,
+        )
+
+    def b_copy(c, h):
+        target = (me_z + n_chunk - c) % n_chunk * pair + (me_c + h) % pair
+        return remote(
+            fin.at[c, h],
+            out_ref.at[me_e],
+            b_send.at[c, h],
+            b_recv.at[c, h],
+            me_s,
+            target,
+        )
+
+    def gather_near(c):
+        for h in range(pair):
+            if c == 0 and h == 0:
+                own.wait()
+            else:
+                z_copy(c, h).wait_recv()
+            for d in range(1, minor):
+                a1_copy(c, h, d).start()
+
+    def gather_far(c):
+        for h in range(pair):
+            for d in range(1, minor):
+                a1_copy(c, h, d).wait_recv()
+            for d in range(1, major):
+                a2_copy(c, h, d).start()
+
+    spans = []
+    for j in range(experts):
+        spans.append((j * slot // 8, -(-(j + 1) * slot // 8)))
+
+    blocks = [(h, i, k) for h in range(pair) for i in range(major) for k in range(minor)]
+
+    def compute(c):
+        for h in range(pair):
+            for d in range(1, major):
+                a2_copy(c, h, d).wait_recv()
+        if c == 0:
+            for copy in weights[:experts]:
+                copy.wait()
+        for j in range(experts):
+            low_g, high_g = spans[j]
+            rows = (high_g - low_g) * 8
+            for b, (h, i, k) in enumerate(blocks):
+                piece = buf[c, h, i, k, low_g:high_g].astype(jnp.float32)
+                xs[j, b * rows : (b + 1) * rows] = piece.reshape(rows, width).astype(jnp.bfloat16)
+        tile = 256 if hidden % 256 == 0 else hidden
+
+        def first(n, carry):
+            cols = pl.ds(pl.multiple_of(n * tile, tile), tile) if tile < hidden else slice(None)
+            for j in range(experts):
+                rows = (spans[j][1] - spans[j][0]) * 8 * len(blocks)
+                acc = jnp.dot(
+                    xs[j, :rows], w1[j, :, cols], preferred_element_type=jnp.float32
+                )
+                acc = acc + b_in_ref[j : j + 1, cols]
+                acc = 0.5 * acc * (1.0 + lax.erf(acc * math.sqrt(0.5)))
+                hs[j, :rows, cols] = acc.astype(jnp.bfloat16)
+            return carry
+
+        lax.fori_loop(0, hidden // tile, first, 0)
+        if c == 0:
+            for copy in weights[experts:]:
+                copy.wait()
+        wide = 256 if width % 256 == 0 else width
+
+        def second(n, carry):
+            cols = pl.ds(pl.multiple_of(n * wide, wide), wide) if wide < width else slice(None)
+            outs = []
+            for j in range(experts):
+                rows = (spans[j][1] - spans[j][0]) * 8 * len(blocks)
+                acc = jnp.dot(
+                    hs[j, :rows], w2[j, :, cols], preferred_element_type=jnp.float32
+                )
+                outs.append(acc.reshape(len(blocks), spans[j][1] - spans[j][0], 8, wide))
+            line = lax.broadcasted_iota(jnp.int32, (8, wide), 0)
+            for b, (h, i, k) in enumerate(blocks):
+                for g in range(groups):
+                    value = None
+                    for j in range(experts):
+                        if spans[j][0] <= g < spans[j][1]:
+                            mine = outs[j][b, g - spans[j][0]]
+                            if value is None:
+                                value = mine
+                            else:
+                                value = jnp.where(line + g * 8 < j * slot, value, mine)
+                    part[c, h, i, k, g, :, cols] = value.astype(jnp.bfloat16)
+            return carry
+
+        lax.fori_loop(0, width // wide, second, 0)
+        for h in range(pair):
+            for d in range(1, major):
+                r1_copy(c, h, d).start()
+
+    def reduce_far(c):
+        for h in range(pair):
+            maj, low = place(h)
+            for d in range(1, major):
+                r1_copy(c, h, d).wait_recv()
+            for k in range(minor):
+                for g in range(groups):
+                    total = part[c, h, maj, k, g].astype(jnp.float32)
+                    for d in range(1, major):
+                        total = total + got1[c, h, d - 1, k, g].astype(jnp.float32)
+                    red[c, h, k, g] = total.astype(jnp.bfloat16)
+            for d in range(1, minor):
+                r2_copy(c, h, d).start()
+
+    def reduce_near(c):
+        line = lax.broadcasted_iota(jnp.int32, (8, width), 0)
+        for h in range(pair):
+            maj, low = place(h)
+            for d in range(1, minor):
+                r2_copy(c, h, d).wait_recv()
+            for g in range(groups):
+                total = red[c, h, low, g].astype(jnp.float32)
+                for d in range(1, minor):
+                    total = total + got2[c, h, d - 1, g].astype(jnp.float32)
+                bias = jnp.broadcast_to(b_out_ref[0:1, :], (8, width))
+                for j in range(1, experts):
+                    bias = jnp.where(line + g * 8 < j * slot, bias, b_out_ref[j : j + 1, :])
+                value = (total + bias).astype(jnp.bfloat16)
+                if c == 0 and h == 0:
+                    out_ref[me_e, g] = value
+                else:
+                    fin[c, h, g] = value
+            if not (c == 0 and h == 0):
+                b_copy(c, h).start()
+
+    own.start()
+    for c in range(n_chunk):
+        for h in range(pair):
+            if not (c == 0 and h == 0):
+                z_copy(c, h).start()
+        if c == 0:
+            for copy in weights:
+                copy.start()
+    stages = ((gather_near, 0), (gather_far, 1), (compute, 2), (reduce_far, 3), (reduce_near, 4))
+    for t in range(n_chunk + 4):
+        for stage, lag in stages:
+            if 0 <= t - lag < n_chunk:
+                stage(t - lag)
+    for c in range(n_chunk):
+        for h in range(pair):
+            if not (c == 0 and h == 0):
+                b_copy(c, h).wait_recv()
+                b_copy(c, h).wait_send()
+                z_copy(c, h).wait_send()
+            for d in range(1, minor):
+                a1_copy(c, h, d).wait_send()
+                r2_copy(c, h, d).wait_send()
+            for d in range(1, major):
+                a2_copy(c, h, d).wait_send()
+                r1_copy(c, h, d).wait_send()
+
+
+def expert_exchange(sent, w_in, b_in, w_out, b_out, n_seq, slot):
+    n_exp, groups, _, width = sent.shape
+    experts, _, hidden = w_in.shape
+    pair = 2 if n_exp % 2 == 0 else 1
+    n_chunk = n_exp // pair
+    side = math.isqrt(n_seq)
+    major, minor = (side, side) if side * side == n_seq else (1, n_seq)
+    dims = (n_seq, n_exp, n_chunk, pair, major, minor, experts, slot)
+    block = (groups, 8, width)
+    bf = jnp.bfloat16
+    tallest = max(-(-(j + 1) * slot // 8) - j * slot // 8 for j in range(experts)) * 8
+    rows = tallest * pair * n_seq
+    sem = pltpu.SemaphoreType.DMA
+    vmem = pl.BlockSpec(memory_space=pltpu.VMEM)
+    hbm = pl.BlockSpec(memory_space=pl.ANY)
+    return pl.pallas_call(
+        functools.partial(exchange_kernel, dims),
+        out_shape=jax.ShapeDtypeStruct(sent.shape, bf),
+        in_specs=[vmem, vmem, vmem, hbm, hbm],
+        out_specs=vmem,
+        scratch_shapes=[
+            pltpu.VMEM(w_in.shape, bf),
+            pltpu.VMEM(w_out.shape, bf),
+            pltpu.VMEM((n_chunk, pair, major, minor) + block, bf),
+            pltpu.VMEM((n_chunk, pair, major, minor) + block, bf),
+            pltpu.VMEM((n_chunk, pair, max(major - 1, 1), minor) + block, bf),
+            pltpu.VMEM((n_chunk, pair, minor) + block, bf),
+            pltpu.VMEM((n_chunk, pair, max(minor - 1, 1)) + block, bf),
+            pltpu.VMEM((n_chunk, pair) + block, bf),
+            pltpu.VMEM((experts, rows, width), bf),
+            pltpu.VMEM((experts, rows, hidden), bf),
+            sem((2, experts)),
+            sem,
+            sem((n_chunk, pair)),
+            sem((n_chunk, pair)),
+            sem((n_chunk, pair, minor)),
+            sem((n_chunk, pair, minor)),
+            sem((n_chunk, pair, major)),
+            sem((n_chunk, pair, major)),
+            sem((n_chunk, pair, major)),
+            sem((n_chunk, pair, major)),
+            sem((n_chunk, pair, minor)),
+            sem((n_chunk, pair, minor)),
+            sem((n_chunk, pair)),
+            sem((n_chunk, pair)),
+        ],
+        compiler_params=pltpu.CompilerParams(
+            collective_id=0, has_side_effects=True, vmem_limit_bytes=VMEM_LIMIT
+        ),
+        cost_estimate=pl.CostEstimate(
+            flops=4 * experts * rows * width * hidden,
+            bytes_accessed=4 * experts * width * hidden,
+            transcendentals=experts * rows * hidden,
+        ),
+    )(sent, b_in, b_out, w_in, w_out)
 
 
 def body(
@@ -72,43 +454,33 @@
     holders = lax.axis_size("exp")
     experts = per_device * holders
     slot_count = 5 * tok_rows // (4 * experts)
+    block_rows = -(-per_device * slot_count // 8) * 8
     route_ids = expert_ids.reshape(tok_rows)
     one_hot = (route_ids[:, None] == jnp.arange(experts, dtype=jnp.int32)[None, :]).astype(
-        jnp.float32
+        jnp.bfloat16
     )
     positions = jnp.arange(tok_rows, dtype=jnp.int32)
-    below_mask = (positions[:, None] > positions[None, :]).astype(jnp.float32)
-    earlier = jnp.dot(below_mask, one_hot, precision=lax.Precision.HIGHEST)
-    slot_rank = jnp.sum(earlier * one_hot, axis=1).astype(jnp.int32)
+    below_mask = (positions[:, None] > positions[None, :]).astype(jnp.bfloat16)
+    earlier = jnp.dot(below_mask, one_hot, preferred_element_type=jnp.float32)
+    slot_rank = jnp.sum(earlier * one_hot.astype(jnp.float32), axis=1).astype(jnp.int32)
     column = (
-        route_ids // per_device * slot_count + slot_rank
-    ) * per_device + route_ids % per_device
+        route_ids // per_device * block_rows + route_ids % per_device * slot_count + slot_rank
+    )
     dispatch_mask = (
-        column[:, None] == jnp.arange(experts * slot_count, dtype=jnp.int32)[None, :]
+        column[:, None] == jnp.arange(holders * block_rows, dtype=jnp.int32)[None, :]
     ).astype(jnp.bfloat16)
     dispatched = jnp.einsum(
         "tk,td->kd", dispatch_mask, expert_in, preferred_element_type=jnp.float32
     ).astype(jnp.bfloat16)
-    dispatched = dispatched.reshape(holders, slot_count, per_device, width_d)
-    received = lax.all_to_all(dispatched, "exp", split_axis=0, concat_axis=0, tiled=True)
-    gathered = lax.all_gather(received, "seq", axis=0, tiled=True)
-    hidden = (
-        jnp.einsum("kcjd,jdf->kcjf", gathered, w_in, preferred_element_type=jnp.float32)
-        + b_in[None, None]
-    )
-    hidden = jax.nn.gelu(hidden, approximate=False).astype(jnp.bfloat16)
-    summed = lax.psum_scatter(
-        jnp.einsum("kcjf,jfd->kcjd", hidden, w_out, preferred_element_type=jnp.float32).astype(
-            jnp.bfloat16
-        ),
-        "seq",
-        scatter_dimension=0,
-        tiled=True,
-    ).astype(jnp.float32)
-    back = (summed + b_out[None, None]).astype(jnp.bfloat16)
-    returned = lax.all_to_all(back, "exp", split_axis=0, concat_axis=0, tiled=True).reshape(
-        experts * slot_count, width_d
-    )
+    returned = expert_exchange(
+        dispatched.reshape(holders, block_rows // 8, 8, width_d),
+        w_in,
+        b_in,
+        w_out,
+        b_out,
+        lax.axis_size("seq"),
+        slot_count,
+    ).reshape(holders * block_rows, width_d)
     combined = jnp.dot(dispatch_mask, returned, preferred_element_type=jnp.float32)
     result = mixed.reshape(tok_rows, width_d) + gate_values.reshape(tok_rows)[:, None] * combined
     return result.astype(jnp.bfloat16).reshape(tokens.shape)

time: 252 us -> 103 us (0.41)
  waiting for transfers between devices: 153 us -> 3.23 us
  Pallas kernels: 0 us -> 81.1 us
  blocking collectives: 27 us -> 0 us
  matrix products: 27.8 us -> 4.14 us
  between operations: 14.2 us -> 0.17 us
  starting transfers between devices: 10.9 us -> 5.37 us
  other arithmetic: 10.5 us -> 5.63 us
  local copies, waits for them, and re-layouts: 6.83 us -> 2.86 us
    unnamed x3 -> x0, waiting for transfers between devices: 88.1 us -> none
    pallas_call x0 -> x1, Pallas kernels: none -> 81.1 us  [expert_exchange(): pl.pallas_call(functools.partial(exchange_kernel, dims), out_shape=jax.Sh...]
    all_gather x1 -> x0, waiting for transfers between devices: 44.4 us -> none  [body(): gathered = lax.all_gather(received, 'seq', axis=0, tiled=True)]
    all_to_all x1 -> x0, blocking collectives: 27 us -> none  [body(): lax.all_to_all(dispatched, 'exp', split_axis=0, concat_axis=0, tiled=True)]
    dot_general x2 -> x1, matrix products: 25.9 us -> 0.2 us  [body(): earlier = jnp.dot(below_mask, one_hot, preferred_element_type=jnp.float32)]
    all_to_all x1 -> x0, waiting for transfers between devices: 20.6 us -> none  [body(): lax.all_to_all(back, 'exp', split_axis=0, concat_axis=0, tiled=True)]
    all_to_all x1 -> x0, starting transfers between devices: 5.44 us -> none  [body(): lax.all_to_all(back, 'exp', split_axis=0, concat_axis=0, tiled=True)]
    ppermute x1, waiting for transfers between devices: 0.01 us -> 3.23 us  [with_halo(): lax.ppermute(head, axis, [((i + 1) % count, i) for i in range(ends)])]
  transfers between devices with their start and end apart: 5 -> 2, of which waited for: 3 -> 1; matrix products, arithmetic and copies ran while one was open for 3% -> 3% of each run, Pallas kernels for 0% -> 0%
where the time goes in v1:
time: 103 us; the launch traced here: 102 us
  Pallas kernels  81.1 us (79%)
  other arithmetic  5.63 us (5%)
  starting transfers between devices  5.37 us (5%)
  matrix products  4.14 us (4%)
  waiting for transfers between devices  3.23 us (3%)
  local copies, waits for them, and re-layouts  2.86 us (3%)
    pallas_call x1, Pallas kernels, expert_exchange(): pl.pallas_call(functools.partial(exchange_kernel, dims), out_shape=jax.Sh...  81.1 us
    ppermute x1, starting transfers between devices, with_halo(): lax.ppermute(tail, axis, [(i, (i + 1) % count) for i in range(ends)])  3.94 us
    ppermute x1, waiting for transfers between devices, with_halo(): lax.ppermute(head, axis, [((i + 1) % count, i) for i in range(ends)])  3.23 us
    reduce_sum x3, other arithmetic, normalize(): row_mean = jnp.mean(values, axis=-1, keepdims=True)  3.15 us
    dot_general x1, matrix products, body(): jnp.dot(dispatch_mask, returned, preferred_element_type=jnp.float32)  2.54 us
  transfers between devices with their start and end apart: 2, of which 1 were waited for; matrix products, arithmetic and copies ran while one was open for 3% of the time, Pallas kernels for 0%

profile of v1, /device:TPU:1, one launch (start us, length us, event | category | flops | bytes accessed | tf_op | source)
XLA Modules:
  0.0 102.5 jit_solution(14608922797971986201)
XLA Ops:
  0.0 1.1 %slice_bitcast_fusion.1 = (bf16[1,64,1280]{2,1,0:T(8,128)(2,1)S(1)}, bf16[1,64,1280]{2,1,0:T(8,128)(2,1)S(1)}) fusion(bf16[1,4,64,1280]{3,2,1,0:T(8,128)(2,1)} %param.11), kind=kLoop, calls=%fused_computation.55 | loop fusion | bytes 655360 | tf_op jit(solution)/shard_map/slice | solution.py:17
  1.1 3.9 %collective-permute-start = (bf16[1,64,1280]{2,1,0:T(8,128)(2,1)S(1)}, bf16[1,64,1280]{2,1,0:T(8,128)(2,1)S(1)}, u32[]{:S(2)}, u32[]{:S(2)}) collective-permute-start(bf16[1,64,1280]{2,1,0:T(8,128)(2,1)S(1)} %get-tuple-element.16), channel_id=1, source_target_pairs={{0,8},{8,16},{16,24},{1,9},{9,17},{17,25},{2,10},{10,18},{18,26},{... | collective-permute-start | bytes 491528 | tf_op jit(solution)/shard_map/ppermute | solution.py:20
  5.1 1.4 %collective-permute-start.1 = (bf16[1,64,1280]{2,1,0:T(8,128)(2,1)S(1)}, bf16[1,64,1280]{2,1,0:T(8,128)(2,1)S(1)}, u32[]{:S(2)}, u32[]{:S(2)}) collective-permute-start(bf16[1,64,1280]{2,1,0:T(8,128)(2,1)S(1)} %get-tuple-element.17), channel_id=1, source_target_pairs={{8,0},{16,8},{24,16},{9,1},{17,9},{25,17},{10,2},{18,10},{26,18},{... | collective-permute-start | bytes 491528 | tf_op jit(solution)/shard_map/ppermute | solution.py:22
  6.5 1.3 %convert_reduce_fusion = f32[4,64]{1,0:T(4,128)S(1)} fusion(bf16[1,4,64,1280]{3,2,1,0:T(8,128)(2,1)} %param.11), kind=kLoop, calls=%fused_computation.10 | loop fusion | flops 655104 | bytes 656384 | tf_op jit(solution)/shard_map/reduce_sum | solution.py:30
  7.8 0.3 fusion.6
  8.1 0.5 broadcast.153
  8.6 0.7 reduce.22
  9.3 0.1 reshape.118
  9.4 0.2 fusion.24
  9.6 0.3 fusion.8
  10.0 0.1 slice_reduce_fusion.8
  10.1 3.2 %collective-permute-done.1 = bf16[1,64,1280]{2,1,0:T(8,128)(2,1)S(1)} collective-permute-done((bf16[1,64,1280]{2,1,0:T(8,128)(2,1)S(1)}, bf16[1,64,1280]{2,1,0:T(8,128)(2,1)S(1)}, u32[]{:S(2)}, u32[]{:S(2)}) %collective-permute-start.1) | collective-permute-done | bytes 163872 | tf_op jit(solution)/shard_map/ppermute | solution.py:22
  13.4 0.1 convert_reduce_fusion.1
  13.5 0.2 fusion.27
  13.7 0.2 fusion.29
  14.0 0.2 maximum_convert_fusion
  14.2 0.5 copy-done.4
  14.7 1.8 %fusion.37 = (f32[4,64]{1,0:T(4,128)S(1)}, f32[4,64,1280]{2,1,0:T(8,128)S(1)}) fusion(f32[1280]{0:T(1024)S(1)} %copy-done.4, f32[1280]{0:T(1024)S(1)} %get-tuple-element.12, f32[1280]{0:T(1024)S(1)} %get-tuple-element.13, f32[6,64,1280]{2,1,0:T(8,128)S(1)} %maximum_convert_fusion, f32[1280]{0:T(1024)S(1)} %get-tuple-element.6, ...), kind=kLoop, calls=%fused_computation.82 | loop fusion | flops 6881024 | bytes 7947264 | tf_op jit(solution)/shard_map/reduce_sum | solution.py:30
  16.5 0.3 multiply_reduce_fusion
  16.8 0.4 copy-done.3
  17.2 0.2 multiply_convert_fusion
  17.4 1.4 %convolution_convert_fusion = bf16[320,1280]{1,0:T(8,128)(2,1)} fusion(bf16[256,1280]{1,0:T(8,128)(2,1)S(1)} %bitcast.34, s32[256]{0:T(256)S(1)} %fusion.36), kind=kOutput, calls=%fused_computation.2 | convolution fusion | flops 210206720 | bytes 1475584 | tf_op jit(solution)/shard_map/tk,td->kd/dot_general | solution.py:472
  18.8 81.1 %shard_map.109 = bf16[8,5,8,1280]{3,2,1,0:T(8,128)(2,1)} custom-call(bf16[8,5,8,1280]{3,2,1,0:T(8,128)(2,1)} %bitcast.33, f32[2,1280]{1,0:T(2,128)} %b_in_ref.1, f32[2,1280]{1,0:T(2,128)} %b_out_ref.1, bf16[2,1280,1280]{2,1,0:T(8,128)(2,1)} %w_in_ref.1, bf16[2,1280,1280]{2,1,0:T(8,128)(2,1)} %w_out_ref.1), custom_call_target="tpu_custom_call" | custom-call | flops 2516582400 | bytes 13107200 | tf_op jit(solution)/shard_map/pallas_call | solution.py:384
  99.9 2.5 %fusion.1 = bf16[256,1280]{1,0:T(8,128)(2,1)} fusion(f32[256,1280]{1,0:T(8,128)S(1)} %bitcast.31, bf16[320,1280]{1,0:T(8,128)(2,1)} %bitcast.32, f32[256]{0:T(256)S(1)} %mul.217, s32[256]{0:T(256)S(1)} %fusion.36), kind=kOutput, calls=%fused_computation.3 | convolution fusion | flops 210780160 | bytes 2787328 | tf_op jit(solution)/shard_map/dot_general | solution.py:484
  (22 shorter events, 0.2 us)
Async XLA Ops:
  0.0 7.8 %copy-start = (bf16[1,4,64,1280]{3,2,1,0:T(8,128)(2,1)S(1)}, bf16[1,4,64,1280]{3,2,1,0:T(8,128)(2,1)}, u32[]{:S(2)}) copy-start(bf16[1,4,64,1280]{3,2,1,0:T(8,128)(2,1)} %param.11) | copy-start | bytes 1966084
  0.0 8.6 %copy-start.6 = (s32[1,4,64,1]{2,3,1,0:T(1,128)S(1)}, s32[1,4,64,1]{2,3,1,0:T(1,128)}, u32[]{:S(2)}) copy-start(s32[1,4,64,1]{2,3,1,0:T(1,128)} %param.12) | copy-start | bytes 3076
  0.0 9.6 %copy-start.2 = (f32[1280]{0:T(1024)S(1)}, f32[1280]{0:T(1024)}, u32[]{:S(2)}) copy-start(f32[1280]{0:T(1024)} %param.14) | copy-start | bytes 15364
  1.1 9.0 %collective-permute-start = (bf16[1,64,1280]{2,1,0:T(8,128)(2,1)S(1)}, bf16[1,64,1280]{2,1,0:T(8,128)(2,1)S(1)}, u32[]{:S(2)}, u32[]{:S(2)}) collective-permute-start(bf16[1,64,1280]{2,1,0:T(8,128)(2,1)S(1)} %get-tuple-element.16), channel_id=1, source_target_pairs={{0,8},{8,16},{16,24},{1,9},{9,17},{17,25},{2,10},{10,18},{18,26},{... | collective-permute-start | bytes 491528 | tf_op jit(solution)/shard_map/ppermute | solution.py:20
  5.0 4.9 %copy-start.5 = (f32[1,4,64]{2,1,0:T(4,128)S(1)}, f32[1,4,64]{2,1,0:T(4,128)}, u32[]{:S(2)}) copy-start(f32[1,4,64]{2,1,0:T(4,128)} %param.13) | copy-start | bytes 3076
  5.1 4.9 %copy-start.1 = (f32[3,3,1280]{2,1,0:T(4,128)S(1)}, f32[3,3,1280]{2,1,0:T(4,128)}, u32[]{:S(2)}) copy-start(f32[3,3,1280]{2,1,0:T(4,128)} %param.16) | copy-start | bytes 138244
  5.1 8.3 %collective-permute-start.1 = (bf16[1,64,1280]{2,1,0:T(8,128)(2,1)S(1)}, bf16[1,64,1280]{2,1,0:T(8,128)(2,1)S(1)}, u32[]{:S(2)}, u32[]{:S(2)}) collective-permute-start(bf16[1,64,1280]{2,1,0:T(8,128)(2,1)S(1)} %get-tuple-element.17), channel_id=1, source_target_pairs={{8,0},{16,8},{24,16},{9,1},{17,9},{25,17},{10,2},{18,10},{26,18},{... | collective-permute-start | bytes 491528 | tf_op jit(solution)/shard_map/ppermute | solution.py:22
  14.0 0.7 copy-start.4
  16.5 0.7 copy-start.3

commit v2 on v1

--- a/solution.py
+++ b/solution.py
@@ -9,55 +9,30 @@
 from jax.sharding import PartitionSpec as P
 
 
-def with_halo(cells, sides, width):
-    for axis, dim in sides:
-        count = lax.axis_size(axis)
-        ends = count - 1
-        head = lax.slice_in_dim(cells, 0, width, axis=dim)
-        tail = lax.slice_in_dim(cells, cells.shape[dim] - width, cells.shape[dim], axis=dim)
-        cells = jnp.concatenate(
-            [
-                lax.ppermute(tail, axis, [(i, (i + 1) % count) for i in range(ends)]),
-                cells,
-                lax.ppermute(head, axis, [((i + 1) % count, i) for i in range(ends)]),
-            ],
-            axis=dim,
-        )
-    return cells
-
-
-def normalize(values, scales):
-    row_mean = jnp.mean(values, axis=-1, keepdims=True)
-    centred = values - row_mean
-    row_var = jnp.mean(centred * centred, axis=-1, keepdims=True)
-    return centred * lax.rsqrt(row_var + 1e-06) * scales
-
-
-def depthwise(padded, conv_weight, height, width):
-    summed = padded[..., 0:height, 0:width, :] * conv_weight[0, 0]
-    for row_off in range(3):
-        for col_off in range(3):
-            if row_off + col_off > 0:
-                summed = (
-                    summed
-                    + padded[..., row_off : row_off + height, col_off : col_off + width, :]
-                    * conv_weight[row_off, col_off]
-                )
-    return summed
-
-
-VMEM_LIMIT = 62 * 1024 * 1024
+VMEM_LIMIT = 67_000_000
 MESH = pl.DeviceIdType.MESH
 
 
 def exchange_kernel(
     dims,
-    x_ref,
+    tok_ref,
+    ids_ref,
+    gain1_ref,
+    gain2_ref,
+    taps_ref,
+    conv_bias_ref,
     b_in_ref,
     b_out_ref,
     w_in_ref,
     w_out_ref,
     out_ref,
+    column_ref,
+    mixed_ref,
+    x_ref,
+    halo,
+    pad,
+    mix,
+    ein,
     w1,
     w2,
     buf,
@@ -65,7 +40,6 @@
     got1,
     red,
     got2,
-    fin,
     xs,
     hs,
     w_sem,
@@ -82,10 +56,13 @@
     r2_recv,
     b_send,
     b_recv,
+    halo_send,
+    halo_recv,
+    mix_sem,
 ):
     n_seq, n_exp, n_chunk, pair, major, minor, experts, slot = dims
-    groups = x_ref.shape[1]
-    width = x_ref.shape[3]
+    groups = out_ref.shape[1]
+    width = out_ref.shape[3]
     hidden = w1.shape[2]
     me_s = lax.axis_index("seq")
     me_e = lax.axis_index("exp")
@@ -147,6 +124,16 @@
                     device_id_type=MESH,
                 )
                 greeted += 1
+    for d in (1, n_seq - 1):
+        pl.semaphore_signal(
+            barrier,
+            inc=1,
+            device_id={"seq": (me_s + d) % n_seq, "exp": me_e},
+            device_id_type=MESH,
+        )
+        greeted += 1
+    for copy in weights:
+        copy.start()
     pl.semaphore_wait(barrier, greeted)
 
     def z_copy(c, h):
@@ -213,7 +200,7 @@
     def b_copy(c, h):
         target = (me_z + n_chunk - c) % n_chunk * pair + (me_c + h) % pair
         return remote(
-            fin.at[c, h],
+            red.at[c, h, place(h)[1]],
             out_ref.at[me_e],
             b_send.at[c, h],
             b_recv.at[c, h],
@@ -300,6 +287,8 @@
             return carry
 
         lax.fori_loop(0, width // wide, second, 0)
+
+    def send_far(c):
         for h in range(pair):
             for d in range(1, major):
                 r1_copy(c, h, d).start()
@@ -335,23 +324,139 @@
                 if c == 0 and h == 0:
                     out_ref[me_e, g] = value
                 else:
-                    fin[c, h, g] = value
+                    red[c, h, low, g] = value
             if not (c == 0 and h == 0):
                 b_copy(c, h).start()
 
-    own.start()
+    row_count, cols = tok_ref.shape[0], tok_ref.shape[1]
+    halos = [
+        remote(
+            tok_ref.at[row_count - 1],
+            halo.at[0],
+            halo_send.at[0],
+            halo_recv.at[0],
+            (me_s + 1) % n_seq,
+            me_e,
+        ),
+        remote(
+            tok_ref.at[0],
+            halo.at[1],
+            halo_send.at[1],
+            halo_recv.at[1],
+            (me_s + n_seq - 1) % n_seq,
+            me_e,
+        ),
+    ]
+    for copy in halos:
+        copy.start()
+
+    step = 16
+
+    def norm(values, scales):
+        mean = jnp.mean(values, axis=-1, keepdims=True)
+        centred = values - mean
+        var = jnp.mean(centred * centred, axis=-1, keepdims=True)
+        return (centred * lax.rsqrt(var + 1e-06) * scales).astype(jnp.bfloat16)
+
+    edge = jnp.zeros((8, width), jnp.float32)
+
+    def norm_row(r, carry):
+        pad[r + 1, 0:8] = edge
+        pad[r + 1, cols + 8 : cols + 16] = edge
+        for q in range(cols // step):
+            piece = tok_ref[r, q * step : (q + 1) * step].astype(jnp.float32)
+            pad[r + 1, 8 + q * step : 8 + (q + 1) * step] = norm(piece, gain1_ref[...]).astype(
+                jnp.float32
+            )
+        return carry
+
+    lax.fori_loop(0, row_count, norm_row, 0)
+
+    def mix_row(r, carry):
+        for q in range(cols // step):
+            total = tok_ref[r, q * step : (q + 1) * step].astype(jnp.float32)
+            total = total + conv_bias_ref[...]
+            for a in range(3):
+                for b in range(3):
+                    low = 7 + b + q * step
+                    tap = taps_ref[3 * a + b : 3 * a + b + 1, :]
+                    total = total + pad[r + a, low : low + step] * tap
+            where = pl.ds(pl.multiple_of(r * cols + q * step, step), step)
+            mix[where, :] = total
+            ein[where, :] = norm(total, gain2_ref[...])
+        return carry
+
+    tok_rows = ids_ref.shape[1]
+    total_experts = experts * n_exp
+    ids = ids_ref[...]
+    names = lax.broadcasted_iota(jnp.int32, (total_experts, tok_rows), 0)
+    one_hot = jnp.where(names == ids, 1.0, 0.0)
+    before = lax.broadcasted_iota(jnp.int32, (tok_rows, tok_rows), 0)
+    after = lax.broadcasted_iota(jnp.int32, (tok_rows, tok_rows), 1)
+    earlier = jnp.dot(
+        one_hot.astype(jnp.bfloat16),
+        jnp.where(before < after, 1.0, 0.0).astype(jnp.bfloat16),
+        preferred_element_type=jnp.float32,
+    )
+    rank = jnp.sum(one_hot * earlier, axis=0, keepdims=True)
+    ids_f = ids.astype(jnp.float32)
+    holder = jnp.floor((ids_f + 0.5) * (1.0 / experts))
+    column = holder * (groups * 8.0) + (ids_f - holder * experts) * (1.0 * slot) + rank
+    column_ref[...] = column
+
+    lax.fori_loop(1, row_count - 1, mix_row, 0)
+    for side, copy in enumerate(halos):
+        copy.wait_recv()
+    ends = (me_s > 0, me_s < n_seq - 1)
+    for side, r in ((0, 0), (1, row_count + 1)):
+        keep = jnp.where(ends[side], 1.0, 0.0).astype(jnp.float32)
+        pad[r, 0:8] = edge
+        pad[r, cols + 8 : cols + 16] = edge
+        for q in range(cols // step):
+            piece = halo[side, q * step : (q + 1) * step].astype(jnp.float32)
+            pad[r, 8 + q * step : 8 + (q + 1) * step] = (
+                norm(piece, gain1_ref[...]).astype(jnp.float32) * keep
+            )
+    for r in range(0, row_count, max(row_count - 1, 1)):
+        mix_row(r, 0)
+    keep_mix = pltpu.make_async_copy(mix, mixed_ref, mix_sem)
+    keep_mix.start()
+
+    height = groups * 8
     for c in range(n_chunk):
-        for h in range(pair):
-            if not (c == 0 and h == 0):
+        targets = [
+            (me_z + c) % n_chunk * pair + (me_c + pair - h) % pair for h in range(pair)
+        ]
+        line = lax.broadcasted_iota(jnp.int32, (pair * height, tok_rows), 0)
+        name = line + targets[0] * height
+        for h in range(1, pair):
+            name = jnp.where(line < h * height, name, line + (targets[h] - h) * height)
+        mask = jnp.where(name.astype(jnp.float32) == column, 1.0, 0.0).astype(jnp.bfloat16)
+        picked = jnp.dot(mask, ein[...], preferred_element_type=jnp.float32)
+        for h in range(pair):
+            piece = picked[h * height : (h + 1) * height].reshape(groups, 8, width)
+            x_ref[targets[h]] = piece.astype(jnp.bfloat16)
+            if c == 0 and h == 0:
+                own.start()
+            else:
                 z_copy(c, h).start()
-        if c == 0:
-            for copy in weights:
-                copy.start()
-    stages = ((gather_near, 0), (gather_far, 1), (compute, 2), (reduce_far, 3), (reduce_near, 4))
-    for t in range(n_chunk + 4):
-        for stage, lag in stages:
-            if 0 <= t - lag < n_chunk:
-                stage(t - lag)
+
+    send_order = list(range(1, n_chunk)) + [0]
+    events = [(0.0, gather_near, 0)]
+    for c in range(1, n_chunk):
+        events.append((c, gather_near, c))
+    for c in range(n_chunk):
+        events.append((c + 0.9, gather_far, c))
+        events.append((c + 2.3, compute, c))
+    for n, c in enumerate(send_order):
+        events.append((n + 3.4 if c else n_chunk + 1.5, send_far, c))
+        events.append((n + 4.5, reduce_far, c))
+        events.append((n + 5.6, reduce_near, c))
+    for _, stage, c in sorted(events, key=lambda event: event[0]):
+        stage(c)
+    keep_mix.wait()
+    for copy in halos:
+        copy.wait_send()
     for c in range(n_chunk):
         for h in range(pair):
             if not (c == 0 and h == 0):
@@ -366,8 +471,10 @@
                 r1_copy(c, h, d).wait_send()
 
 
-def expert_exchange(sent, w_in, b_in, w_out, b_out, n_seq, slot):
-    n_exp, groups, _, width = sent.shape
+def expert_exchange(front, w_in, b_in, w_out, b_out, n_seq, n_exp, slot):
+    row_count, cols, width = front[0].shape
+    tok_rows = row_count * cols
+    groups = -(-w_in.shape[0] * slot // 8)
     experts, _, hidden = w_in.shape
     pair = 2 if n_exp % 2 == 0 else 1
     n_chunk = n_exp // pair
@@ -383,10 +490,19 @@
     hbm = pl.BlockSpec(memory_space=pl.ANY)
     return pl.pallas_call(
         functools.partial(exchange_kernel, dims),
-        out_shape=jax.ShapeDtypeStruct(sent.shape, bf),
-        in_specs=[vmem, vmem, vmem, hbm, hbm],
-        out_specs=vmem,
+        out_shape=(
+            jax.ShapeDtypeStruct((n_exp,) + block, bf),
+            jax.ShapeDtypeStruct((1, tok_rows), jnp.float32),
+            jax.ShapeDtypeStruct((tok_rows, width), jnp.float32),
+        ),
+        in_specs=[vmem] * 8 + [hbm, hbm],
+        out_specs=(vmem, vmem, hbm),
         scratch_shapes=[
+            pltpu.VMEM((n_exp,) + block, bf),
+            pltpu.VMEM((2, cols, width), bf),
+            pltpu.VMEM((row_count + 2, cols + 16, width), jnp.float32),
+            pltpu.VMEM((tok_rows, width), jnp.float32),
+            pltpu.VMEM((tok_rows, width), bf),
             pltpu.VMEM(w_in.shape, bf),
             pltpu.VMEM(w_out.shape, bf),
             pltpu.VMEM((n_chunk, pair, major, minor) + block, bf),
@@ -394,7 +510,6 @@
             pltpu.VMEM((n_chunk, pair, max(major - 1, 1), minor) + block, bf),
             pltpu.VMEM((n_chunk, pair, minor) + block, bf),
             pltpu.VMEM((n_chunk, pair, max(minor - 1, 1)) + block, bf),
-            pltpu.VMEM((n_chunk, pair) + block, bf),
             pltpu.VMEM((experts, rows, width), bf),
             pltpu.VMEM((experts, rows, hidden), bf),
             sem((2, experts)),
@@ -411,6 +526,9 @@
             sem((n_chunk, pair, minor)),
             sem((n_chunk, pair)),
             sem((n_chunk, pair)),
+            sem((2,)),
+            sem((2,)),
+            sem,
         ],
         compiler_params=pltpu.CompilerParams(
             collective_id=0, has_side_effects=True, vmem_limit_bytes=VMEM_LIMIT
@@ -420,7 +538,7 @@
             bytes_accessed=4 * experts * width * hidden,
             transcendentals=experts * rows * hidden,
         ),
-    )(sent, b_in, b_out, w_in, w_out)
+    )(*front, b_in, b_out, w_in, w_out)
 
 
 def body(
@@ -439,48 +557,28 @@
     row_count = tokens.shape[1]
     col_count = tokens.shape[2]
     width_d = tokens.shape[3]
-    values = tokens[0].astype(jnp.float32)
-    normed = normalize(values, mixer_gain).astype(jnp.bfloat16)
-    rim_source = tokens[0]
-    extended = with_halo(rim_source, (("seq", 0),), 1)
-    rim_rows = jnp.concatenate([extended[0:1], extended[row_count + 1 : row_count + 2]], axis=0)
-    rim_rows = normalize(rim_rows.astype(jnp.float32), mixer_gain).astype(jnp.bfloat16)
-    extended = jnp.concatenate([rim_rows[0:1], normed, rim_rows[1:2]], axis=0)
-    padded = jnp.pad(extended.astype(jnp.float32), ((0, 0), (1, 1), (0, 0)))
-    mixed = values + depthwise(padded, conv_weight, row_count, col_count) + conv_bias
     tok_rows = row_count * col_count
-    expert_in = normalize(mixed, expert_gain).astype(jnp.bfloat16).reshape(tok_rows, width_d)
     per_device = w_in.shape[0]
     holders = lax.axis_size("exp")
     experts = per_device * holders
     slot_count = 5 * tok_rows // (4 * experts)
     block_rows = -(-per_device * slot_count // 8) * 8
-    route_ids = expert_ids.reshape(tok_rows)
-    one_hot = (route_ids[:, None] == jnp.arange(experts, dtype=jnp.int32)[None, :]).astype(
-        jnp.bfloat16
+    front = (
+        tokens[0],
+        expert_ids.reshape(1, tok_rows),
+        mixer_gain.reshape(1, width_d),
+        expert_gain.reshape(1, width_d),
+        conv_weight.reshape(9, width_d),
+        conv_bias.reshape(1, width_d),
     )
-    positions = jnp.arange(tok_rows, dtype=jnp.int32)
-    below_mask = (positions[:, None] > positions[None, :]).astype(jnp.bfloat16)
-    earlier = jnp.dot(below_mask, one_hot, preferred_element_type=jnp.float32)
-    slot_rank = jnp.sum(earlier * one_hot.astype(jnp.float32), axis=1).astype(jnp.int32)
-    column = (
-        route_ids // per_device * block_rows + route_ids % per_device * slot_count + slot_rank
+    returned, column, mixed = expert_exchange(
+        front, w_in, b_in, w_out, b_out, lax.axis_size("seq"), holders, slot_count
     )
+    returned = returned.reshape(holders * block_rows, width_d)
     dispatch_mask = (
-        column[:, None] == jnp.arange(holders * block_rows, dtype=jnp.int32)[None, :]
+        column.reshape(tok_rows)[:, None]
+        == jnp.arange(holders * block_rows, dtype=jnp.float32)[None, :]
     ).astype(jnp.bfloat16)
-    dispatched = jnp.einsum(
-        "tk,td->kd", dispatch_mask, expert_in, preferred_element_type=jnp.float32
-    ).astype(jnp.bfloat16)
-    returned = expert_exchange(
-        dispatched.reshape(holders, block_rows // 8, 8, width_d),
-        w_in,
-        b_in,
-        w_out,
-        b_out,
-        lax.axis_size("seq"),
-        slot_count,
-    ).reshape(holders * block_rows, width_d)
     combined = jnp.dot(dispatch_mask, returned, preferred_element_type=jnp.float32)
     result = mixed.reshape(tok_rows, width_d) + gate_values.reshape(tok_rows)[:, None] * combined
     return result.astype(jnp.bfloat16).reshape(tokens.shape)

time: 103 us -> 99 us (0.961)
  Pallas kernels: 81.1 us -> 87 us
  starting transfers between devices: 5.37 us -> 0 us
  local copies, waits for them, and re-layouts: 2.86 us -> 7.28 us
  other arithmetic: 5.63 us -> 1.34 us
  waiting for transfers between devices: 3.23 us -> 0 us
  matrix products: 4.14 us -> 2.96 us
    pallas_call x1, Pallas kernels: 81.1 us -> 87 us  [expert_exchange(): pl.pallas_call(functools.partial(exchange_kernel, dims), out_shape=(jax.S...]
    reshape x1 -> x5, local copies, waits for them, and re-layouts: 0.08 us -> 6.01 us  [the longest x1 1.49 us: body(): conv_weight.reshape(9, width_d)]
    ppermute x2 -> x0, starting transfers between devices: 5.37 us -> none  [the longest x1 3.94 us: with_halo(): lax.ppermute(tail, axis, [(i, (i + 1) % count) for i in range(ends)])]
    reduce_sum x6 -> x0, other arithmetic: 3.98 us -> none  [the longest x3 3.15 us: normalize(): row_mean = jnp.mean(values, axis=-1, keepdims=True)]
    ppermute x2 -> x0, waiting for transfers between devices: 3.23 us -> none  [the longest x1 3.23 us: with_halo(): lax.ppermute(head, axis, [((i + 1) % count, i) for i in range(ends)])]
    dot_general x2 -> x0, matrix products: 1.6 us -> none  [the longest x1 1.4 us: body(): jnp.einsum('tk,td->kd', dispatch_mask, expert_in, preferred_element_type=...]
    slice x3 -> x0, local copies, waits for them, and re-layouts: 1.23 us -> none  [the longest x1 1.08 us: with_halo(): lax.slice_in_dim(cells, cells.shape[dim] - width, cells.shape[dim], axis=...]
  transfers between devices with their start and end apart: 2 -> 0, of which waited for: 1 -> 0; matrix products, arithmetic and copies ran while one was open for 3% -> 0% of each run, Pallas kernels for 0% -> 0%
where the time goes in v2:
time: 99 us; the launch traced here: 98.6 us
  Pallas kernels  87 us (88%)
  local copies, waits for them, and re-layouts  7.28 us (7%)
  matrix products  2.96 us (3%)
  other arithmetic  1.34 us (1%)
    pallas_call x1, Pallas kernels, expert_exchange(): pl.pallas_call(functools.partial(exchange_kernel, dims), out_shape=(jax.S...  87 us
    dot_general x1, matrix products, body(): jnp.dot(dispatch_mask, returned, preferred_element_type=jnp.float32)  2.96 us

profile of v2, /device:TPU:1, one launch (start us, length us, event | category | flops | bytes accessed | tf_op | source)
XLA Modules:
  0.0 98.6 jit_solution(17877977199860658918)
XLA Ops:
  0.0 0.8 mul.10
  0.8 0.5 broadcast.3
  1.3 1.3 %reduce.3 = s32[4,64]{1,0:T(4,128)S(1)} reduce(s32[1,4,64,1]{2,3,1,0:T(1,128)} %param.12, s32[]{:T(128)} %broadcast.3), dimensions={0,3}, to_apply=%param.12.reduce_sub_computation.3 | reduce | bytes 2052 | tf_op args[1]
  2.6 0.6 reshape.23.ids_ref
  3.3 1.3 %reshape.24.gain1_ref = f32[1,1280]{1,0:T(1,128)} reshape(f32[1280]{0:T(1024)} %param.14) | data formatting | bytes 10240 | tf_op jit(solution)/shard_map/reshape | solution.py:569
  4.6 1.3 %reshape.25.gain2_ref = f32[1,1280]{1,0:T(1,128)} reshape(f32[1280]{0:T(1024)} %param.15) | data formatting | bytes 10240 | tf_op jit(solution)/shard_map/reshape | solution.py:570
  5.8 1.3 %reshape.27.conv_bias_ref = f32[1,1280]{1,0:T(1,128)} reshape(f32[1280]{0:T(1024)} %param.17) | data formatting | bytes 10240 | tf_op jit(solution)/shard_map/reshape | solution.py:572
  7.1 1.5 %reshape.26.taps_ref = f32[9,1280]{1,0:T(8,128)} reshape(f32[3,3,1280]{2,1,0:T(4,128)} %param.16) | data formatting | bytes 92160 | tf_op jit(solution)/shard_map/reshape | solution.py:571
  8.6 87.0 %shard_map.109 = (bf16[8,5,8,1280]{3,2,1,0:T(8,128)(2,1)}, f32[1,256]{1,0:T(1,128)}, f32[256,1280]{1,0:T(8,128)}) custom-call(bf16[4,64,1280]{2,1,0:T(8,128)(2,1)} %bitcast.7, s32[1,256]{1,0:T(1,128)} %reshape.23.ids_ref, f32[1,1280]{1,0:T(1,128)} %reshape.24.gain1_ref, f32[1,1280]{1,0:T(1,128)} %reshape.25.gain2_ref, f32[9,1280]{1,0:T(8,128)} %reshape.26.taps_ref, ...), custom_call_target="tpu_custom_call" | custom-call | flops 2516582400 | bytes 13107200 | tf_op jit(solution)/shard_map/pallas_call | solution.py:491
  95.7 3.0 %fusion.1 = bf16[256,1280]{1,0:T(8,128)(2,1)} fusion(f32[256,1280]{1,0:T(8,128)} %get-tuple-element.8, bf16[320,1280]{1,0:T(8,128)(2,1)} %bitcast.6, f32[256]{0:T(256)S(1)} %mul.10, f32[256]{0:T(256)} %bitcast.8), kind=kOutput, calls=%fused_computation.2 | convolution fusion | flops 210780160 | bytes 2787328 | tf_op jit(solution)/shard_map/dot_general | solution.py:582
